TPU v7x, 128 devices: a whole 4x4x4 slice. The times are simulated.
128 devices in a mesh: row: 16 (over y, z), col: 8 (over x, core).
Axes of the slice: x: 4, y: 4, z: 4, core: 2. Of those that a mesh axis runs over, the one named last changes fastest.
Arguments:
- grid_values: bfloat16 [512, 256, 384], P(('row', 'col')), may hold values from -0.109375 to 0.109375
- external: float32 [512, 256], P(('row', 'col')), may hold values from 0 to 6
- tiles: int32 [512, 3], P(('row', 'col')), may hold values from 0 to 15, as said below
- kinetic: bfloat16 [16384, 16384], P('row', 'col'), may hold values from -0.046875 to 0.046875
- orbitals: bfloat16 [16384, 256], P(('row', 'col')), may hold values from -6 to 6
Outputs:
- filtered: float32 [16384, 256], P(('row', 'col'))
Inputs may be any that keep to these rules, and one draw needn't show every extreme that they name: Each batch names 3 distinct tiles in increasing order. Among the 4 batches of one device no tile is named more than 2 times; in every draw some tile is named exactly 2 times by the batches of every device.
All inputs are finite; a program needn't handle non-finite values.
Results may differ from a plain program's by a relative error of at most 0.0064.
Values may be sent and summed in bfloat16 or wider, within the bound.
A program may use at most 128 MiB of HBM per device.

v0:
```python
import jax
import jax.numpy as jnp
from jax import lax
from jax.sharding import PartitionSpec as P

TILE = 128
LISTED = 3
LIST = 384
center = 1.0
spread = 2.5


def body(grid_values, external, tiles, kinetic, orbitals):
    row_count = lax.axis_size("row")
    shard_rows, orbital_count = orbitals.shape
    per_shard = shard_rows // TILE
    group_tiles = row_count * per_shard
    batch_count = tiles.shape[0]
    group_orbitals = lax.all_gather(orbitals, "row", axis=0, tiled=True)
    listed_orbitals = group_orbitals.reshape(group_tiles, TILE, orbital_count)[tiles].reshape(
        batch_count, LIST, orbital_count
    )
    waves = jnp.einsum(
        "bpl,blk->bpk", grid_values, listed_orbitals, preferred_element_type=jnp.float32
    )
    density = jnp.sum(waves * waves, axis=2)
    potential = external - jnp.cbrt(3.0 * density / jnp.pi)
    weighted = (potential[:, :, None] * grid_values).astype(jnp.bfloat16)
    integrals = jnp.einsum(
        "bpl,bpm->blm", grid_values, weighted, preferred_element_type=jnp.float32
    )
    blocks = integrals.reshape(batch_count, LISTED, TILE, LISTED, TILE).transpose(0, 1, 3, 2, 4)
    dense_local = (
        jnp.zeros((group_tiles, TILE, group_tiles, TILE), jnp.float32)
        .at[tiles[:, :, None], :, tiles[:, None, :], :]
        .add(blocks)
    )
    dense_local = dense_local.reshape(group_tiles * TILE, group_tiles * TILE)
    grid_rows = lax.psum_scatter(dense_local, "row", scatter_dimension=0, tiled=True)
    row_start = lax.axis_index("col") * shard_rows
    updated = (
        lax.dynamic_slice_in_dim(kinetic, row_start, shard_rows, 0).astype(jnp.float32) + grid_rows
    )
    hamiltonian = lax.dynamic_update_slice_in_dim(
        kinetic, updated.astype(jnp.bfloat16), row_start, 0
    )

    def add_piece(piece):
        return jnp.dot(hamiltonian, piece, preferred_element_type=jnp.float32)

    def times_ham(vectors):
        return add_piece(lax.all_gather(vectors, "row", axis=0, tiled=True))

    def filter_step(partial_value, vectors):
        reduced = lax.psum_scatter(partial_value, "col", scatter_dimension=0, tiled=True)
        return reduced / spread - center / spread * vectors.astype(jnp.float32)

    first_term = filter_step(
        jnp.dot(hamiltonian, group_orbitals, preferred_element_type=jnp.float32), orbitals
    ).astype(jnp.bfloat16)
    second_term = (
        2.0 * filter_step(times_ham(first_term), first_term) - orbitals.astype(jnp.float32)
    ).astype(jnp.bfloat16)
    return 2.0 * filter_step(times_ham(second_term), second_term) - first_term.astype(jnp.float32)


def solution(mesh):
    return jax.shard_map(
        body,
        mesh=mesh,
        in_specs=(
            P(("row", "col"), None, None),
            P(("row", "col"), None),
            P(("row", "col"), None),
            P("row", "col"),
            P(("row", "col"), None),
        ),
        out_specs=P(("row", "col"), None),
        check_vma=False,
    )
```

profile of v0, /device:TPU:0, one launch (start us, length us, event | category | flops | bytes accessed | tf_op | source)
XLA Modules:
  0.0 429.0 jit_solution(10878357735825306583)
XLA Ops:
  6.5 0.0 all-gather.4.cloned.1.call-start
  6.5 4.8 %copy.28 = bf16[1024,2048]{1,0:T(8,128)(2,1)} copy(bf16[1024,2048]{1,0:T(8,128)(2,1)} %param.8) | data formatting | bytes 8388608
  11.3 0.0 all-gather.4.cloned.1.call-update
  11.4 0.0 reduce-scatter.5.cloned.1.call-start
  11.4 0.0 copy-done.5
  11.5 0.1 or_select_fusion
  11.5 0.1 reshape.38
  11.6 0.1 reshape.32
  11.7 44.9 %all-gather.4.cloned.1.call-done = bf16[2048,256]{1,0:T(8,128)(2,1)} async-done(((bf16[128,256]{1,0:T(8,128)(2,1)}), bf16[2048,256]{1,0:T(8,128)(2,1)}) %all-gather.4.cloned.1.call-update) | async-done | bytes 1048592 | tf_op jit(solution)/shard_map/all_gather | solution.py:19
  56.7 1.8 gather_fusion
  58.5 0.0 copy-done
  58.5 0.5 fusion
  59.0 0.0 copy-done.6
  59.0 0.9 convolution_bitcast_fusion
  60.0 2.0 copy.17
  62.0 4.5 %reshape.28 = f32[4,3,128,3,128]{4,3,2,1,0:T(4,128)} reshape(f32[4,384,384]{2,1,0:T(8,128)} %copy.17) | data formatting | bytes 4718592 | tf_op jit(solution)/shard_map/reshape | solution.py:32
  66.5 2.2 copy.18
  68.7 7.9 %broadcast_in_dim.8 = f32[16,128,16,128]{3,1,2,0:T(8,128)} broadcast(f32[]{:T(128)} %constant.13.clone.1), dimensions={} | broadcast | bytes 16777220 | tf_op jit(solution)/shard_map/broadcast_in_dim | solution.py:34
  76.6 9.1 %scatter_fusion = f32[16,128,16,128]{3,1,2,0:T(8,128)} fusion(f32[16,128,16,128]{3,1,2,0:T(8,128)} %broadcast_in_dim.8, s32[36]{0:T(128)S(1)} %reshape.38, f32[36,128,128]{2,1,0:T(8,128)S(1)} %bitcast.24), kind=kCustom, calls=%fused_computation.1 | custom fusion | flops 589824 | bytes 7078176 | tf_op jit(solution)/shard_map/scatter-add | solution.py:36
  85.7 15.5 %copy.19 = f32[16,128,16,128]{3,2,1,0:T(8,128)S(1)} copy(f32[16,128,16,128]{3,1,2,0:T(8,128)} %scatter_fusion) | data formatting | bytes 33554432 | tf_op jit(solution)/shard_map/scatter-add | solution.py:36
  101.2 11.2 %copy.24 = f32[256,8,16,128]{3,1,2,0:T(8,128)} copy(f32[256,8,16,128]{3,2,1,0:T(8,128)S(1)} %bitcast.23) | data formatting | bytes 33554432
  112.4 0.0 reduce-scatter.5.cloned.1.call-update
  112.4 0.2 reduce-scatter.7.cloned.1.call-start
  112.6 110.1 %reduce-scatter.5.cloned.1.call-done = f32[128,2048]{1,0:T(8,128)} async-done(((f32[2048,2048]{1,0:T(8,128)}), f32[128,2048]{1,0:T(8,128)}) %reduce-scatter.5.cloned.1.call-update) | async-done | bytes 1048592 | tf_op jit(solution)/shard_map/reduce_scatter | solution.py:39
  222.8 2.3 fusion.2
  225.1 4.4 %fusion.8 = f32[1024,256]{1,0:T(8,128)} fusion(bf16[1024,2048]{1,0:T(8,128)(2,1)} %fusion.2, bf16[2048,256]{1,0:T(8,128)(2,1)S(1)} %copy-done.2), kind=kOutput, calls=%fused_computation.26 | convolution fusion | flops 1073741824 | bytes 6291456 | tf_op jit(solution)/shard_map/dot_general | solution.py:59
  229.5 0.0 reduce-scatter.7.cloned.1.call-update
  229.5 0.0 all-gather.6.cloned.1.call-start
  229.6 31.5 %reduce-scatter.7.cloned.1.call-done = f32[128,256]{1,0:T(8,128)} async-done(((f32[1024,256]{1,0:T(8,128)}), f32[128,256]{1,0:T(8,128)}) %reduce-scatter.7.cloned.1.call-update) | async-done | bytes 131088 | tf_op jit(solution)/shard_map/reduce_scatter | solution.py:55
  261.1 1.6 fusion.4
  262.6 0.0 all-gather.6.cloned.1.call-update
  262.6 0.0 copy-start.1
  262.7 0.0 reduce-scatter.9.cloned.1.call-start
  262.7 41.8 %all-gather.6.cloned.1.call-done = bf16[2048,256]{1,0:T(8,128)(2,1)} async-done(((bf16[128,256]{1,0:T(8,128)(2,1)}), bf16[2048,256]{1,0:T(8,128)(2,1)}) %all-gather.6.cloned.1.call-update) | async-done | bytes 1048592 | tf_op jit(solution)/shard_map/all_gather | solution.py:52
  304.5 4.7 %fusion.9 = f32[1024,256]{1,0:T(8,128)} fusion(bf16[1024,2048]{1,0:T(8,128)(2,1)} %fusion.2, bf16[2048,256]{1,0:T(8,128)(2,1)} %all-gather.6.cloned.1.call-done), kind=kOutput, calls=%fused_computation.27 | convolution fusion | flops 1073741824 | bytes 6291456 | tf_op jit(solution)/shard_map/dot_general | solution.py:49
  309.2 0.0 reduce-scatter.9.cloned.1.call-update
  309.3 0.0 all-gather.8.cloned.1.call-start
  309.3 31.5 %reduce-scatter.9.cloned.1.call-done = f32[128,256]{1,0:T(8,128)} async-done(((f32[1024,256]{1,0:T(8,128)}), f32[128,256]{1,0:T(8,128)}) %reduce-scatter.9.cloned.1.call-update) | async-done | bytes 131088 | tf_op jit(solution)/shard_map/reduce_scatter | solution.py:55
  340.8 0.0 copy-done.1
  340.8 1.6 fusion.5
  342.4 0.0 all-gather.8.cloned.1.call-update
  342.4 0.0 copy-start.4
  342.4 0.0 reduce-scatter.11.cloned.1.call-start
  342.5 41.9 %all-gather.8.cloned.1.call-done = bf16[2048,256]{1,0:T(8,128)(2,1)} async-done(((bf16[128,256]{1,0:T(8,128)(2,1)}), bf16[2048,256]{1,0:T(8,128)(2,1)}) %all-gather.8.cloned.1.call-update) | async-done | bytes 1048592 | tf_op jit(solution)/shard_map/all_gather | solution.py:52
  384.3 4.7 %fusion.10 = f32[1024,256]{1,0:T(8,128)} fusion(bf16[1024,2048]{1,0:T(8,128)(2,1)} %fusion.2, bf16[2048,256]{1,0:T(8,128)(2,1)} %all-gather.8.cloned.1.call-done), kind=kOutput, calls=%fused_computation.28 | convolution fusion | flops 1073741824 | bytes 6291456 | tf_op jit(solution)/shard_map/dot_general | solution.py:49
  389.0 0.0 reduce-scatter.11.cloned.1.call-update
  389.1 31.5 %reduce-scatter.11.cloned.1.call-done = f32[128,256]{1,0:T(8,128)} async-done(((f32[1024,256]{1,0:T(8,128)}), f32[128,256]{1,0:T(8,128)}) %reduce-scatter.11.cloned.1.call-update) | async-done | bytes 131088 | tf_op jit(solution)/shard_map/reduce_scatter | solution.py:55
  420.6 1.6 convert_subtract_fusion
  (12 shorter events, 0.1 us)
Async XLA Ops:
  6.5 4.9 %copy-start.5 = (s32[4,3]{1,0:T(4,128)S(1)}, s32[4,3]{1,0:T(4,128)}, u32[]{:S(2)}) copy-start(s32[4,3]{1,0:T(4,128)} %param.7) | copy-start | bytes 148
  6.5 52.0 %copy-start = (bf16[4,256,384]{2,1,0:T(8,128)(2,1)S(1)}, bf16[4,256,384]{2,1,0:T(8,128)(2,1)}, u32[]{:S(2)}) copy-start(bf16[4,256,384]{2,1,0:T(8,128)(2,1)} %param.5) | copy-start | bytes 2359300
  6.5 52.5 %copy-start.6 = (f32[4,256]{1,0:T(4,128)S(1)}, f32[4,256]{1,0:T(4,128)}, u32[]{:S(2)}) copy-start(f32[4,256]{1,0:T(4,128)} %param.6) | copy-start | bytes 12292
  6.5 50.1 %all-gather.4.cloned.1.call-start = ((), (), s32[]{:S(2)}) async-start(), calls=%async_computation.4 | async-start | bytes 1114112 | tf_op jit(solution)/shard_map/all_gather | solution.py:19
  11.4 211.4 %reduce-scatter.5.cloned.1.call-start = ((), (), s32[]{:S(2)}) async-start(), calls=%async_computation.5 | async-start | bytes 17825792 | tf_op jit(solution)/shard_map/reduce_scatter | solution.py:39
  112.4 112.7 %copy-start.2 = (bf16[2048,256]{1,0:T(8,128)(2,1)S(1)}, bf16[2048,256]{1,0:T(8,128)(2,1)}, u32[]{:S(2)}) copy-start(bf16[2048,256]{1,0:T(8,128)(2,1)} %all-gather.4.cloned.1.call-done) | copy-start | bytes 3145732
  112.4 148.7 %reduce-scatter.7.cloned.1.call-start = ((), (), s32[]{:S(2)}) async-start(), calls=%async_computation.6 | async-start | bytes 1179648 | tf_op jit(solution)/shard_map/reduce_scatter | solution.py:55
  225.0 36.0 %copy-start.3 = (bf16[128,256]{1,0:T(8,128)(2,1)S(1)}, bf16[128,256]{1,0:T(8,128)(2,1)}, u32[]{:S(2)}) copy-start(bf16[128,256]{1,0:T(8,128)(2,1)} %param.9) | copy-start | bytes 196612
  229.5 75.0 %all-gather.6.cloned.1.call-start = ((), (), s32[]{:S(2)}) async-start(), calls=%async_computation.7 | async-start | bytes 1114112 | tf_op jit(solution)/shard_map/all_gather | solution.py:52
  262.6 78.2 %copy-start.1 = (bf16[128,256]{1,0:T(8,128)(2,1)S(1)}, bf16[128,256]{1,0:T(8,128)(2,1)}, u32[]{:S(2)}) copy-start(bf16[128,256]{1,0:T(8,128)(2,1)} %fusion.4) | copy-start | bytes 196612
  262.7 78.1 %reduce-scatter.9.cloned.1.call-start = ((), (), s32[]{:S(2)}) async-start(), calls=%async_computation.8 | async-start | bytes 1179648 | tf_op jit(solution)/shard_map/reduce_scatter | solution.py:55
  309.3 75.1 %all-gather.8.cloned.1.call-start = ((), (), s32[]{:S(2)}) async-start(), calls=%async_computation.9 | async-start | bytes 1114112 | tf_op jit(solution)/shard_map/all_gather | solution.py:52
  342.4 78.2 %copy-start.4 = (bf16[128,256]{1,0:T(8,128)(2,1)S(1)}, bf16[128,256]{1,0:T(8,128)(2,1)}, u32[]{:S(2)}) copy-start(bf16[128,256]{1,0:T(8,128)(2,1)} %fusion.5) | copy-start | bytes 196612
  342.4 78.2 %reduce-scatter.11.cloned.1.call-start = ((), (), s32[]{:S(2)}) async-start(), calls=%async_computation.10 | async-start | bytes 1179648 | tf_op jit(solution)/shard_map/reduce_scatter | solution.py:55
Sparse Core Ops, SparseCore 0:
  11.5 45.1 all-gather.3
  112.5 110.1 reduce-scatter.4
  229.6 31.3 reduce-scatter.6
  263.1 41.4 all-gather.5
  309.4 31.3 reduce-scatter.8
  342.8 41.4 all-gather.7
  389.2 31.3 reduce-scatter.10
where the time goes:
time: 430 us; the launch traced here: 429 us
  waiting for transfers between devices  333 us (77%)
  local copies, waits for them, and re-layouts  50.1 us (12%)
  other arithmetic  16.3 us (4%)
  matrix products  15.3 us (4%)
  between operations  13.6 us (3%)
    reduce_scatter x1, waiting for transfers between devices, body(): lax.psum_scatter(dense_local, 'row', scatter_dimension=0, tiled=True)  110 us
    reduce_scatter x3, waiting for transfers between devices, filter_step(): lax.psum_scatter(partial_value, 'col', scatter_dimension=0, tiled=True)  94.5 us
    all_gather x2, waiting for transfers between devices, times_ham(): return add_piece(lax.all_gather(vectors, 'row', axis=0, tiled=True))  83.7 us
    all_gather x1, waiting for transfers between devices, body(): group_orbitals = lax.all_gather(orbitals, 'row', axis=0, tiled=True)  44.9 us
    unnamed x16, local copies, waits for them, and re-layouts  16 us
    scatter-add x1, local copies, waits for them, and re-layouts, body(): dense_local = jnp.zeros((group_tiles, TILE, group_tiles, TILE), jnp.float...  15.5 us
    dot_general x2, matrix products, add_piece(): return jnp.dot(hamiltonian, piece, preferred_element_type=jnp.float32)  9.42 us
    scatter-add x1, other arithmetic, body(): dense_local = jnp.zeros((group_tiles, TILE, group_tiles, TILE), jnp.float...  9.12 us
  transfers between devices with their start and end apart: 7, of which 7 were waited for; matrix products, arithmetic and copies ran while one was open for 0% of the time, Pallas kernels for 0%

commit v1 on v0

--- a/solution.py
+++ b/solution.py
@@ -16,7 +16,24 @@
     per_shard = shard_rows // TILE
     group_tiles = row_count * per_shard
     batch_count = tiles.shape[0]
-    group_orbitals = lax.all_gather(orbitals, "row", axis=0, tiled=True)
+
+    def mark_desk(comm_axis, field_in, array_axis=0):
+        n_all = lax.axis_size(comm_axis)
+        samples = tuple(((at, (at + 1) % n_all) for at in range(n_all)))
+        pile = tuple(((at, (at - 1) % n_all) for at in range(n_all)))
+        g_now, m_next = ([field_in], [field_in])
+        for _ in range(n_all // 2):
+            g_now.append(lax.ppermute(g_now[-1], axis_name=comm_axis, perm=samples))
+        for _ in tuple(range((n_all - 1) // 2)):
+            m_next.append(lax.ppermute(m_next[-1], axis_name=comm_axis, perm=pile))
+        x_now = jnp.concatenate([*g_now[::-1], *m_next[1:]], array_axis)
+        return jnp.roll(
+            x_now,
+            shift=(lax.axis_index(comm_axis) - n_all // 2) * field_in.shape[array_axis],
+            axis=array_axis,
+        )
+
+    group_orbitals = mark_desk("row", orbitals)
     listed_orbitals = group_orbitals.reshape(group_tiles, TILE, orbital_count)[tiles].reshape(
         batch_count, LIST, orbital_count
     )

time: 430 us -> 450 us (1.047)
  starting transfers between devices: 0.43 us -> 40.2 us
  waiting for transfers between devices: 333 us -> 313 us
    all_gather x1 -> x0, waiting for transfers between devices: 44.9 us -> none  [body(): group_orbitals = lax.all_gather(orbitals, 'row', axis=0, tiled=True)]
    ppermute x0 -> x15, starting transfers between devices: none -> 40 us  [the longest x7 37.9 us: mark_desk(): m_next.append(lax.ppermute(m_next[-1], axis_name=comm_axis, perm=pile))]
    ppermute x0 -> x15, waiting for transfers between devices: none -> 22.2 us  [the longest x8 22.2 us: mark_desk(): g_now.append(lax.ppermute(g_now[-1], axis_name=comm_axis, perm=samples))]
    unnamed x16 -> x45, local copies, waits for them, and re-layouts: 16 us -> 16.5 us
  transfers between devices with their start and end apart: 7 -> 21, of which waited for: 7 -> 14; matrix products, arithmetic and copies ran while one was open for 0% -> 0% of each run, Pallas kernels for 0% -> 0%
where the time goes in v1:
time: 450 us; the launch traced here: 449 us
  waiting for transfers between devices  313 us (70%)
  local copies, waits for them, and re-layouts  49.4 us (11%)
  starting transfers between devices  40.2 us (9%)
  matrix products  16.7 us (4%)
  other arithmetic  16.4 us (4%)
  between operations  13.9 us (3%)
    reduce_scatter x1, waiting for transfers between devices, body(): lax.psum_scatter(dense_local, 'row', scatter_dimension=0, tiled=True)  112 us
    reduce_scatter x3, waiting for transfers between devices, filter_step(): lax.psum_scatter(partial_value, 'col', scatter_dimension=0, tiled=True)  94.4 us
    all_gather x2, waiting for transfers between devices, times_ham(): return add_piece(lax.all_gather(vectors, 'row', axis=0, tiled=True))  84 us
    ppermute x7, starting transfers between devices, mark_desk(): m_next.append(lax.ppermute(m_next[-1], axis_name=comm_axis, perm=pile))  37.9 us
    ppermute x8, waiting for transfers between devices, mark_desk(): g_now.append(lax.ppermute(g_now[-1], axis_name=comm_axis, perm=samples))  22.2 us
    unnamed x45, local copies, waits for them, and re-layouts  16.5 us
    scatter-add x1, local copies, waits for them, and re-layouts, body(): dense_local = jnp.zeros((group_tiles, TILE, group_tiles, TILE), jnp.float...  15.5 us
    dot_general x2, matrix products, add_piece(): return jnp.dot(hamiltonian, piece, preferred_element_type=jnp.float32)  9.48 us
  transfers between devices with their start and end apart: 21, of which 14 were waited for; matrix products, arithmetic and copies ran while one was open for 0% of the time, Pallas kernels for 0%

profile of v1, /device:TPU:0, one launch (start us, length us, event | category | flops | bytes accessed | tf_op | source)
XLA Modules:
  0.0 449.5 jit_solution(17173363061983561110)
XLA Ops:
  6.5 4.7 %copy.59 = bf16[1024,2048]{1,0:T(8,128)(2,1)} copy(bf16[1024,2048]{1,0:T(8,128)(2,1)} %param.8) | data formatting | bytes 8388608
  11.3 2.0 collective-permute-start
  13.3 6.8 %collective-permute-done = bf16[128,256]{1,0:T(8,128)(2,1)S(1)} collective-permute-done((bf16[128,256]{1,0:T(8,128)(2,1)S(1)}, bf16[128,256]{1,0:T(8,128)(2,1)S(1)}, u32[]{:S(2)}, u32[]{:S(2)}) %collective-permute-start) | collective-permute-done | bytes 65568 | tf_op jit(solution)/shard_map/ppermute | solution.py:26
  20.1 5.3 %collective-permute-start.8 = (bf16[128,256]{1,0:T(8,128)(2,1)S(1)}, bf16[128,256]{1,0:T(8,128)(2,1)S(1)}, u32[]{:S(2)}, u32[]{:S(2)}) collective-permute-start(bf16[128,256]{1,0:T(8,128)(2,1)S(1)} %copy-done.1), channel_id=1, source_target_pairs={{0,120},{8,0},{16,8},{24,16},{32,24},{40,32},{48,40},{56,48},{64,5... | collective-permute-start | bytes 196616 | tf_op jit(solution)/shard_map/ppermute | solution.py:28
  25.5 2.2 collective-permute-done.1
  27.7 5.3 %collective-permute-start.9 = (bf16[128,256]{1,0:T(8,128)(2,1)S(1)}, bf16[128,256]{1,0:T(8,128)(2,1)S(1)}, u32[]{:S(2)}, u32[]{:S(2)}) collective-permute-start(bf16[128,256]{1,0:T(8,128)(2,1)S(1)} %collective-permute-done.8), channel_id=1, source_target_pairs={{0,120},{8,0},{16,8},{24,16},{32,24},{40,32},{48,40},{56,48},{64,5... | collective-permute-start | bytes 196616 | tf_op jit(solution)/shard_map/ppermute | solution.py:28
  33.1 2.2 collective-permute-done.2
  35.3 5.3 %collective-permute-start.10 = (bf16[128,256]{1,0:T(8,128)(2,1)S(1)}, bf16[128,256]{1,0:T(8,128)(2,1)S(1)}, u32[]{:S(2)}, u32[]{:S(2)}) collective-permute-start(bf16[128,256]{1,0:T(8,128)(2,1)S(1)} %collective-permute-done.9), channel_id=1, source_target_pairs={{0,120},{8,0},{16,8},{24,16},{32,24},{40,32},{48,40},{56,48},{64,5... | collective-permute-start | bytes 196616 | tf_op jit(solution)/shard_map/ppermute | solution.py:28
  40.6 2.2 collective-permute-done.3
  42.9 5.4 %collective-permute-start.11 = (bf16[128,256]{1,0:T(8,128)(2,1)S(1)}, bf16[128,256]{1,0:T(8,128)(2,1)S(1)}, u32[]{:S(2)}, u32[]{:S(2)}) collective-permute-start(bf16[128,256]{1,0:T(8,128)(2,1)S(1)} %collective-permute-done.10), channel_id=1, source_target_pairs={{0,120},{8,0},{16,8},{24,16},{32,24},{40,32},{48,40},{56,48},{64,5... | collective-permute-start | bytes 196616 | tf_op jit(solution)/shard_map/ppermute | solution.py:28
  48.3 2.1 collective-permute-done.4
  50.5 5.4 %collective-permute-start.12 = (bf16[128,256]{1,0:T(8,128)(2,1)S(1)}, bf16[128,256]{1,0:T(8,128)(2,1)S(1)}, u32[]{:S(2)}, u32[]{:S(2)}) collective-permute-start(bf16[128,256]{1,0:T(8,128)(2,1)S(1)} %collective-permute-done.11), channel_id=1, source_target_pairs={{0,120},{8,0},{16,8},{24,16},{32,24},{40,32},{48,40},{56,48},{64,5... | collective-permute-start | bytes 196616 | tf_op jit(solution)/shard_map/ppermute | solution.py:28
  55.9 2.7 collective-permute-done.5
  58.6 0.1 or_select_fusion
  58.7 0.1 reshape.32
  58.8 0.1 reshape.38
  58.9 5.4 %collective-permute-start.13 = (bf16[128,256]{1,0:T(8,128)(2,1)S(1)}, bf16[128,256]{1,0:T(8,128)(2,1)S(1)}, u32[]{:S(2)}, u32[]{:S(2)}) collective-permute-start(bf16[128,256]{1,0:T(8,128)(2,1)S(1)} %collective-permute-done.12), channel_id=1, source_target_pairs={{0,120},{8,0},{16,8},{24,16},{32,24},{40,32},{48,40},{56,48},{64,5... | collective-permute-start | bytes 196616 | tf_op jit(solution)/shard_map/ppermute | solution.py:28
  64.3 1.9 collective-permute-done.6
  66.2 5.7 %collective-permute-start.14 = (bf16[128,256]{1,0:T(8,128)(2,1)S(1)}, bf16[128,256]{1,0:T(8,128)(2,1)S(1)}, u32[]{:S(2)}, u32[]{:S(2)}) collective-permute-start(bf16[128,256]{1,0:T(8,128)(2,1)S(1)} %collective-permute-done.13), channel_id=1, source_target_pairs={{0,120},{8,0},{16,8},{24,16},{32,24},{40,32},{48,40},{56,48},{64,5... | collective-permute-start | bytes 196616 | tf_op jit(solution)/shard_map/ppermute | solution.py:28
  71.9 1.9 collective-permute-done.7
  74.2 0.1 constant_dynamic-slice_fusion
  74.3 0.6 gather_fusion
  74.9 0.4 copy-done
  75.3 0.5 fusion
  75.9 2.3 convolution_bitcast_fusion
  78.2 2.0 copy.17
  80.2 4.6 %reshape.28 = f32[4,3,128,3,128]{4,3,2,1,0:T(4,128)} reshape(f32[4,384,384]{2,1,0:T(8,128)} %copy.17) | data formatting | bytes 4718592 | tf_op jit(solution)/shard_map/reshape | solution.py:49
  84.7 2.2 copy.18
  86.9 7.9 %broadcast_in_dim.8 = f32[16,128,16,128]{3,1,2,0:T(8,128)} broadcast(f32[]{:T(128)} %constant.51.clone.1), dimensions={} | broadcast | bytes 16777220 | tf_op jit(solution)/shard_map/broadcast_in_dim | solution.py:51
  94.8 9.3 %scatter_fusion = f32[16,128,16,128]{3,1,2,0:T(8,128)} fusion(f32[16,128,16,128]{3,1,2,0:T(8,128)} %broadcast_in_dim.8, s32[36]{0:T(128)S(1)} %reshape.38, f32[36,128,128]{2,1,0:T(8,128)S(1)} %bitcast.24), kind=kCustom, calls=%fused_computation.1 | custom fusion | flops 589824 | bytes 7078176 | tf_op jit(solution)/shard_map/scatter-add | solution.py:53
  104.0 15.5 %copy.19 = f32[16,128,16,128]{3,2,1,0:T(8,128)S(1)} copy(f32[16,128,16,128]{3,1,2,0:T(8,128)} %scatter_fusion) | data formatting | bytes 33554432 | tf_op jit(solution)/shard_map/scatter-add | solution.py:53
  119.5 11.2 %copy.24 = f32[256,8,16,128]{3,1,2,0:T(8,128)} copy(f32[256,8,16,128]{3,2,1,0:T(8,128)S(1)} %bitcast.23) | data formatting | bytes 33554432
  130.7 0.0 reduce-scatter.7.cloned.1.call-start
  130.8 112.1 %reduce-scatter.5.cloned.1.call-done = f32[128,2048]{1,0:T(8,128)} async-done(((f32[2048,2048]{1,0:T(8,128)}), f32[128,2048]{1,0:T(8,128)}) %reduce-scatter.5.cloned.1.call-update) | async-done | bytes 1048592 | tf_op jit(solution)/shard_map/reduce_scatter | solution.py:56
  242.9 2.3 fusion.2
  245.2 4.4 fusion.8
  249.7 31.4 %reduce-scatter.7.cloned.1.call-done = f32[128,256]{1,0:T(8,128)} async-done(((f32[1024,256]{1,0:T(8,128)}), f32[128,256]{1,0:T(8,128)}) %reduce-scatter.7.cloned.1.call-update) | async-done | bytes 131088 | tf_op jit(solution)/shard_map/reduce_scatter | solution.py:72
  281.1 1.6 fusion.4
  282.7 0.0 reduce-scatter.9.cloned.1.call-start
  282.8 42.1 %all-gather.3.cloned.1.call-done = bf16[2048,256]{1,0:T(8,128)(2,1)} async-done(((bf16[128,256]{1,0:T(8,128)(2,1)}), bf16[2048,256]{1,0:T(8,128)(2,1)}) %all-gather.3.cloned.1.call-update) | async-done | bytes 1048592 | tf_op jit(solution)/shard_map/all_gather | solution.py:69
  324.8 4.7 %fusion.9 = f32[1024,256]{1,0:T(8,128)} fusion(bf16[1024,2048]{1,0:T(8,128)(2,1)} %fusion.2, bf16[2048,256]{1,0:T(8,128)(2,1)} %all-gather.3.cloned.1.call-done), kind=kOutput, calls=%fused_computation.60 | convolution fusion | flops 1073741824 | bytes 6291456 | tf_op jit(solution)/shard_map/dot_general | solution.py:66
  329.6 0.0 all-gather.5.cloned.1.call-start
  329.6 31.5 %reduce-scatter.9.cloned.1.call-done = f32[128,256]{1,0:T(8,128)} async-done(((f32[1024,256]{1,0:T(8,128)}), f32[128,256]{1,0:T(8,128)}) %reduce-scatter.9.cloned.1.call-update) | async-done | bytes 131088 | tf_op jit(solution)/shard_map/reduce_scatter | solution.py:72
  361.1 1.6 fusion.5
  362.8 41.9 %all-gather.5.cloned.1.call-done = bf16[2048,256]{1,0:T(8,128)(2,1)} async-done(((bf16[128,256]{1,0:T(8,128)(2,1)}), bf16[2048,256]{1,0:T(8,128)(2,1)}) %all-gather.5.cloned.1.call-update) | async-done | bytes 1048592 | tf_op jit(solution)/shard_map/all_gather | solution.py:69
  404.7 4.7 %fusion.10 = f32[1024,256]{1,0:T(8,128)} fusion(bf16[1024,2048]{1,0:T(8,128)(2,1)} %fusion.2, bf16[2048,256]{1,0:T(8,128)(2,1)} %all-gather.5.cloned.1.call-done), kind=kOutput, calls=%fused_computation.61 | convolution fusion | flops 1073741824 | bytes 6291456 | tf_op jit(solution)/shard_map/dot_general | solution.py:66
  409.5 31.5 %reduce-scatter.11.cloned.1.call-done = f32[128,256]{1,0:T(8,128)} async-done(((f32[1024,256]{1,0:T(8,128)}), f32[128,256]{1,0:T(8,128)}) %reduce-scatter.11.cloned.1.call-update) | async-done | bytes 131088 | tf_op jit(solution)/shard_map/reduce_scatter | solution.py:72
  441.0 1.6 convert_subtract_fusion
  (70 shorter events, 0.5 us)
Async XLA Ops:
  6.5 4.7 %copy-start.1 = (bf16[128,256]{1,0:T(8,128)(2,1)S(1)}, bf16[128,256]{1,0:T(8,128)(2,1)}, u32[]{:S(2)}) copy-start(bf16[128,256]{1,0:T(8,128)(2,1)} %param.9) | copy-start | bytes 196612
  6.5 36.4 %copy-start.4 = (s32[4,3]{1,0:T(4,128)S(1)}, s32[4,3]{1,0:T(4,128)}, u32[]{:S(2)}) copy-start(s32[4,3]{1,0:T(4,128)} %param.7) | copy-start | bytes 148
  6.5 236.4 %reduce-scatter.5.cloned.1.call-start = ((), (), s32[]{:S(2)}) async-start(), calls=%async_computation.4 | async-start | bytes 17825792 | tf_op jit(solution)/shard_map/reduce_scatter | solution.py:56
  11.3 8.8 %collective-permute-start = (bf16[128,256]{1,0:T(8,128)(2,1)S(1)}, bf16[128,256]{1,0:T(8,128)(2,1)S(1)}, u32[]{:S(2)}, u32[]{:S(2)}) collective-permute-start(bf16[128,256]{1,0:T(8,128)(2,1)S(1)} %copy-done.1), channel_id=1, source_target_pairs={{0,8},{8,16},{16,24},{24,32},{32,40},{40,48},{48,56},{56,64},{64,7... | collective-permute-start | bytes 196616 | tf_op jit(solution)/shard_map/ppermute | solution.py:26
  20.1 7.6 %collective-permute-start.1 = (bf16[128,256]{1,0:T(8,128)(2,1)S(1)}, bf16[128,256]{1,0:T(8,128)(2,1)S(1)}, u32[]{:S(2)}, u32[]{:S(2)}) collective-permute-start(bf16[128,256]{1,0:T(8,128)(2,1)S(1)} %collective-permute-done), channel_id=1, source_target_pairs={{0,8},{8,16},{16,24},{24,32},{32,40},{40,48},{48,56},{56,64},{64,7... | collective-permute-start | bytes 196616 | tf_op jit(solution)/shard_map/ppermute | solution.py:26
  20.1 7.6 %collective-permute-start.8 = (bf16[128,256]{1,0:T(8,128)(2,1)S(1)}, bf16[128,256]{1,0:T(8,128)(2,1)S(1)}, u32[]{:S(2)}, u32[]{:S(2)}) collective-permute-start(bf16[128,256]{1,0:T(8,128)(2,1)S(1)} %copy-done.1), channel_id=1, source_target_pairs={{0,120},{8,0},{16,8},{24,16},{32,24},{40,32},{48,40},{56,48},{64,5... | collective-permute-start | bytes 196616 | tf_op jit(solution)/shard_map/ppermute | solution.py:28
  27.7 7.6 %collective-permute-start.2 = (bf16[128,256]{1,0:T(8,128)(2,1)S(1)}, bf16[128,256]{1,0:T(8,128)(2,1)S(1)}, u32[]{:S(2)}, u32[]{:S(2)}) collective-permute-start(bf16[128,256]{1,0:T(8,128)(2,1)S(1)} %collective-permute-done.1), channel_id=1, source_target_pairs={{0,8},{8,16},{16,24},{24,32},{32,40},{40,48},{48,56},{56,64},{64,7... | collective-permute-start | bytes 196616 | tf_op jit(solution)/shard_map/ppermute | solution.py:26
  27.7 7.6 %collective-permute-start.9 = (bf16[128,256]{1,0:T(8,128)(2,1)S(1)}, bf16[128,256]{1,0:T(8,128)(2,1)S(1)}, u32[]{:S(2)}, u32[]{:S(2)}) collective-permute-start(bf16[128,256]{1,0:T(8,128)(2,1)S(1)} %collective-permute-done.8), channel_id=1, source_target_pairs={{0,120},{8,0},{16,8},{24,16},{32,24},{40,32},{48,40},{56,48},{64,5... | collective-permute-start | bytes 196616 | tf_op jit(solution)/shard_map/ppermute | solution.py:28
  35.3 7.6 %collective-permute-start.3 = (bf16[128,256]{1,0:T(8,128)(2,1)S(1)}, bf16[128,256]{1,0:T(8,128)(2,1)S(1)}, u32[]{:S(2)}, u32[]{:S(2)}) collective-permute-start(bf16[128,256]{1,0:T(8,128)(2,1)S(1)} %collective-permute-done.2), channel_id=1, source_target_pairs={{0,8},{8,16},{16,24},{24,32},{32,40},{40,48},{48,56},{56,64},{64,7... | collective-permute-start | bytes 196616 | tf_op jit(solution)/shard_map/ppermute | solution.py:26
  35.3 7.6 %collective-permute-start.10 = (bf16[128,256]{1,0:T(8,128)(2,1)S(1)}, bf16[128,256]{1,0:T(8,128)(2,1)S(1)}, u32[]{:S(2)}, u32[]{:S(2)}) collective-permute-start(bf16[128,256]{1,0:T(8,128)(2,1)S(1)} %collective-permute-done.9), channel_id=1, source_target_pairs={{0,120},{8,0},{16,8},{24,16},{32,24},{40,32},{48,40},{56,48},{64,5... | collective-permute-start | bytes 196616 | tf_op jit(solution)/shard_map/ppermute | solution.py:28
  42.9 7.6 %collective-permute-start.4 = (bf16[128,256]{1,0:T(8,128)(2,1)S(1)}, bf16[128,256]{1,0:T(8,128)(2,1)S(1)}, u32[]{:S(2)}, u32[]{:S(2)}) collective-permute-start(bf16[128,256]{1,0:T(8,128)(2,1)S(1)} %collective-permute-done.3), channel_id=1, source_target_pairs={{0,8},{8,16},{16,24},{24,32},{32,40},{40,48},{48,56},{56,64},{64,7... | collective-permute-start | bytes 196616 | tf_op jit(solution)/shard_map/ppermute | solution.py:26
  42.9 7.6 %collective-permute-start.11 = (bf16[128,256]{1,0:T(8,128)(2,1)S(1)}, bf16[128,256]{1,0:T(8,128)(2,1)S(1)}, u32[]{:S(2)}, u32[]{:S(2)}) collective-permute-start(bf16[128,256]{1,0:T(8,128)(2,1)S(1)} %collective-permute-done.10), channel_id=1, source_target_pairs={{0,120},{8,0},{16,8},{24,16},{32,24},{40,32},{48,40},{56,48},{64,5... | collective-permute-start | bytes 196616 | tf_op jit(solution)/shard_map/ppermute | solution.py:28
  50.5 8.1 %collective-permute-start.5 = (bf16[128,256]{1,0:T(8,128)(2,1)S(1)}, bf16[128,256]{1,0:T(8,128)(2,1)S(1)}, u32[]{:S(2)}, u32[]{:S(2)}) collective-permute-start(bf16[128,256]{1,0:T(8,128)(2,1)S(1)} %collective-permute-done.4), channel_id=1, source_target_pairs={{0,8},{8,16},{16,24},{24,32},{32,40},{40,48},{48,56},{56,64},{64,7... | collective-permute-start | bytes 196616 | tf_op jit(solution)/shard_map/ppermute | solution.py:26
  50.5 8.4 %collective-permute-start.12 = (bf16[128,256]{1,0:T(8,128)(2,1)S(1)}, bf16[128,256]{1,0:T(8,128)(2,1)S(1)}, u32[]{:S(2)}, u32[]{:S(2)}) collective-permute-start(bf16[128,256]{1,0:T(8,128)(2,1)S(1)} %collective-permute-done.11), channel_id=1, source_target_pairs={{0,120},{8,0},{16,8},{24,16},{32,24},{40,32},{48,40},{56,48},{64,5... | collective-permute-start | bytes 196616 | tf_op jit(solution)/shard_map/ppermute | solution.py:28
  58.6 7.6 %collective-permute-start.6 = (bf16[128,256]{1,0:T(8,128)(2,1)S(1)}, bf16[128,256]{1,0:T(8,128)(2,1)S(1)}, u32[]{:S(2)}, u32[]{:S(2)}) collective-permute-start(bf16[128,256]{1,0:T(8,128)(2,1)S(1)} %collective-permute-done.5), channel_id=1, source_target_pairs={{0,8},{8,16},{16,24},{24,32},{32,40},{40,48},{48,56},{56,64},{64,7... | collective-permute-start | bytes 196616 | tf_op jit(solution)/shard_map/ppermute | solution.py:26
  58.9 7.3 %collective-permute-start.13 = (bf16[128,256]{1,0:T(8,128)(2,1)S(1)}, bf16[128,256]{1,0:T(8,128)(2,1)S(1)}, u32[]{:S(2)}, u32[]{:S(2)}) collective-permute-start(bf16[128,256]{1,0:T(8,128)(2,1)S(1)} %collective-permute-done.12), channel_id=1, source_target_pairs={{0,120},{8,0},{16,8},{24,16},{32,24},{40,32},{48,40},{56,48},{64,5... | collective-permute-start | bytes 196616 | tf_op jit(solution)/shard_map/ppermute | solution.py:28
  66.2 7.6 %collective-permute-start.7 = (bf16[128,256]{1,0:T(8,128)(2,1)S(1)}, bf16[128,256]{1,0:T(8,128)(2,1)S(1)}, u32[]{:S(2)}, u32[]{:S(2)}) collective-permute-start(bf16[128,256]{1,0:T(8,128)(2,1)S(1)} %collective-permute-done.6), channel_id=1, source_target_pairs={{0,8},{8,16},{16,24},{24,32},{32,40},{40,48},{48,56},{56,64},{64,7... | collective-permute-start | bytes 196616 | tf_op jit(solution)/shard_map/ppermute | solution.py:26
  66.2 7.8 %collective-permute-start.14 = (bf16[128,256]{1,0:T(8,128)(2,1)S(1)}, bf16[128,256]{1,0:T(8,128)(2,1)S(1)}, u32[]{:S(2)}, u32[]{:S(2)}) collective-permute-start(bf16[128,256]{1,0:T(8,128)(2,1)S(1)} %collective-permute-done.13), channel_id=1, source_target_pairs={{0,120},{8,0},{16,8},{24,16},{32,24},{40,32},{48,40},{56,48},{64,5... | collective-permute-start | bytes 196616 | tf_op jit(solution)/shard_map/ppermute | solution.py:28
  74.2 1.1 copy-start
  74.3 1.5 copy-start.5
  130.7 150.4 %reduce-scatter.7.cloned.1.call-start = ((), (), s32[]{:S(2)}) async-start(), calls=%async_computation.5 | async-start | bytes 1179648 | tf_op jit(solution)/shard_map/reduce_scatter | solution.py:72
  249.7 75.2 %all-gather.3.cloned.1.call-start = ((), (), s32[]{:S(2)}) async-start(), calls=%async_computation.6 | async-start | bytes 1114112 | tf_op jit(solution)/shard_map/all_gather | solution.py:69
  282.7 78.4 %copy-start.2 = (bf16[128,256]{1,0:T(8,128)(2,1)S(1)}, bf16[128,256]{1,0:T(8,128)(2,1)}, u32[]{:S(2)}) copy-start(bf16[128,256]{1,0:T(8,128)(2,1)} %fusion.4) | copy-start | bytes 196612
  282.7 78.4 %reduce-scatter.9.cloned.1.call-start = ((), (), s32[]{:S(2)}) async-start(), calls=%async_computation.7 | async-start | bytes 1179648 | tf_op jit(solution)/shard_map/reduce_scatter | solution.py:72
  329.6 75.1 %all-gather.5.cloned.1.call-start = ((), (), s32[]{:S(2)}) async-start(), calls=%async_computation.8 | async-start | bytes 1114112 | tf_op jit(solution)/shard_map/all_gather | solution.py:69
  362.7 78.3 %copy-start.3 = (bf16[128,256]{1,0:T(8,128)(2,1)S(1)}, bf16[128,256]{1,0:T(8,128)(2,1)}, u32[]{:S(2)}) copy-start(bf16[128,256]{1,0:T(8,128)(2,1)} %fusion.5) | copy-start | bytes 196612
  362.8 78.3 %reduce-scatter.11.cloned.1.call-start = ((), (), s32[]{:S(2)}) async-start(), calls=%async_computation.9 | async-start | bytes 1179648 | tf_op jit(solution)/shard_map/reduce_scatter | solution.py:72
Sparse Core Ops, SparseCore 0:
  130.8 112.0 reduce-scatter.4
  249.8 31.2 reduce-scatter.6
  283.3 41.5 all-gather.2
  329.7 31.3 reduce-scatter.8
  363.1 41.5 all-gather.4
  409.6 31.3 reduce-scatter.10
